TPU v7x, 32 devices: a whole 2x2x4 slice. The times are simulated.
32 devices in a mesh: tilt: 2 (over y), row: 8 (over z, x), col: 2 (over core).
Axes of the slice: x: 2, y: 2, z: 4, core: 2. Of those that a mesh axis runs over, the one named last changes fastest.
Arguments:
- object_field: float32 [2, 2048, 256], P(None, ('tilt', 'row'), 'col'), parts along dimension 1, may hold values from -4.2 to 4.2
- probe: float32 [8, 2, 128, 128], P('tilt'), parts along dimension 0, may hold values from -2.1 to 2.1
- patterns: float32 [16, 2, 2, 128, 128], P(('tilt', 'row'), 'col'), parts along dimension 0, may hold values from 0.1 to 3
- offsets: int32 [16, 2, 2, 2], P(('tilt', 'row'), 'col'), parts along dimension 0, may hold values from 0 to 256
- counts: int32 [16, 2], P(('tilt', 'row'), 'col'), parts along dimension 0, may hold values from 1 to 2, as said below
Outputs:
- object_out: float32 [2, 2048, 256], P(None, ('tilt', 'row'), 'col'), parts along dimension 1
- probe_out: float32 [8, 2, 128, 128], P('tilt'), parts along dimension 0
There are 2 independent parts, one for each index of `tilt`. A program takes and returns all parts, laid end to end along the dimension named above; each array names one. Nothing has to cross between parts.
Inputs may be any that keep to these rules, and one draw needn't show every extreme that they name: Only the first counts[r, c] slots of a tile are live; some tile has all 2 live. `offsets`: A window lies inside its tile's frame of 384 pixels a side.
All inputs are finite; a program needn't handle non-finite values.
Results may differ from a plain program's by a relative error of at most 0.0003.
Values sent between devices are 32-bit elements; how exact they have to be, the bound alone decides.
A program may use at most 64 MiB of HBM per device.

v0:
```python
import jax
import jax.numpy as jnp
from jax import lax
from jax.sharding import PartitionSpec as P

H = 128
object_rate = 1.0
probe_rate = 1.0
epsilon = 1e-06


def with_halo(block, sides, width):
    for axis, dim in sides:
        count = lax.axis_size(axis)
        forward = [(i, i + 1) for i in range(count - 1)]
        backward = [(target, source) for source, target in forward]
        low = lax.ppermute(
            lax.slice_in_dim(block, block.shape[dim] - width, None, axis=dim), axis, forward
        )
        high = lax.ppermute(lax.slice_in_dim(block, 0, width, axis=dim), axis, backward)
        block = jnp.concatenate([low, block, high], axis=dim)
    return block


def as_index(value):
    return jnp.asarray(value).astype(jnp.int32)


def dft_tables(length):
    counter = jnp.arange(length, dtype=jnp.int32)
    product = counter[:, None] * counter[None, :] % length
    angle = -2.0 * jnp.pi / length * product.astype(jnp.float32)
    norm = 1.0 / jnp.sqrt(jnp.float32(length))
    return (jnp.cos(angle) * norm, jnp.sin(angle) * norm)


def left_product(cos_table, sin_table, real_part, imag_part):
    hp = lax.Precision.HIGHEST
    real_out = jnp.einsum("ab,kbc->kac", cos_table, real_part, precision=hp) - jnp.einsum(
        "ab,kbc->kac", sin_table, imag_part, precision=hp
    )
    imag_out = jnp.einsum("ab,kbc->kac", cos_table, imag_part, precision=hp) + jnp.einsum(
        "ab,kbc->kac", sin_table, real_part, precision=hp
    )
    return (real_out, imag_out)


def right_product(real_part, imag_part, cos_table, sin_table):
    hp = lax.Precision.HIGHEST
    real_out = jnp.einsum("kab,bc->kac", real_part, cos_table, precision=hp) - jnp.einsum(
        "kab,bc->kac", imag_part, sin_table, precision=hp
    )
    imag_out = jnp.einsum("kab,bc->kac", real_part, sin_table, precision=hp) + jnp.einsum(
        "kab,bc->kac", imag_part, cos_table, precision=hp
    )
    return (real_out, imag_out)


def transform(real_part, imag_part, cos_table, sin_table):
    middle_re, middle_im = left_product(cos_table, sin_table, real_part, imag_part)
    return right_product(middle_re, middle_im, cos_table, sin_table)


def slot_terms(window, probe, pattern, cos_table, sin_table):
    window_re, window_im = (window[0], window[1])
    probe_re, probe_im = (probe[:, 0], probe[:, 1])
    exit_re = probe_re * window_re - probe_im * window_im
    exit_im = probe_re * window_im + probe_im * window_re
    far_re, far_im = transform(exit_re, exit_im, cos_table, sin_table)
    intensity = jnp.sum(far_re * far_re + far_im * far_im, axis=0)
    misfit = intensity - pattern
    back_re, back_im = transform(misfit * far_re, misfit * far_im, cos_table, -sin_table)
    grad_re = jnp.sum(probe_re * back_re + probe_im * back_im, axis=0)
    grad_im = jnp.sum(probe_re * back_im - probe_im * back_re, axis=0)
    term_re = window_re * back_re + window_im * back_im
    term_im = window_re * back_im - window_im * back_re
    return (jnp.stack([grad_re, grad_im]), jnp.stack([term_re, term_im], axis=1))


def body(object_field, probe, patterns, offsets, counts):
    width = probe.shape[-1]
    block = object_field.shape[1]
    slot_total = patterns.shape[2]
    cos_table, sin_table = dft_tables(width)
    tile_total = lax.axis_size("row") * lax.axis_size("col")
    live_count = counts[0, 0]
    frame = with_halo(object_field, (("row", 1), ("col", 2)), H)

    def slot_step(slot_index, inner):
        local_grad, probe_acc = inner
        slot_index = as_index(slot_index)
        corner_y = as_index(offsets[0, 0, slot_index, 0])
        corner_x = as_index(offsets[0, 0, slot_index, 1])
        window = lax.dynamic_slice(frame, (as_index(0), corner_y, corner_x), (2, width, width))
        window_grad, probe_term = slot_terms(
            window, probe, patterns[0, 0, slot_index], cos_table, sin_table
        )
        live = (slot_index < live_count).astype(jnp.float32)
        region = (
            lax.dynamic_slice(local_grad, (as_index(0), corner_y, corner_x), (2, width, width))
            + live * window_grad
        )
        local_grad = lax.dynamic_update_slice(local_grad, region, (as_index(0), corner_y, corner_x))
        return (local_grad, probe_acc + live * probe_term)

    start_carry = (jnp.zeros_like(frame), jnp.zeros_like(probe))
    gradient, probe_grad = lax.fori_loop(0, slot_total, slot_step, start_carry)
    upper_strip = gradient[:, :H, :]
    lower_strip = gradient[:, H + block :, :]
    middle = gradient[:, H : H + block, :]
    row_edges = jnp.concatenate([upper_strip, lower_strip], axis=1)
    row_grown = with_halo(row_edges, (("row", 1),), H)
    from_above = row_grown[:, :H, :]
    from_below = row_grown[:, 3 * H :, :]
    middle = middle.at[:, :H, :].add(from_above).at[:, block - H :, :].add(from_below)
    left_strip = middle[:, :, :H]
    right_strip = middle[:, :, H + block :]
    object_grad = middle[:, :, H : H + block]
    col_edges = jnp.concatenate([left_strip, right_strip], axis=2)
    col_grown = with_halo(col_edges, (("col", 2),), H)
    from_left = col_grown[:, :, :H]
    from_right = col_grown[:, :, 3 * H :]
    object_grad = object_grad.at[:, :, :H].add(from_left).at[:, :, block - H :].add(from_right)
    weight = (
        jnp.max(jnp.sum(probe[:, 0] * probe[:, 0] + probe[:, 1] * probe[:, 1], axis=0)) + epsilon
    )
    object_field = object_field - object_rate * object_grad / weight
    summed = lax.psum(probe_grad, ("row", "col"))
    probe = probe - probe_rate * summed / tile_total
    return (object_field, probe)


def solution(mesh):
    placed = (
        P(None, ("tilt", "row"), "col"),
        P("tilt", None, None, None),
        P(("tilt", "row"), "col", None, None, None),
        P(("tilt", "row"), "col", None, None),
        P(("tilt", "row"), "col"),
    )
    return jax.shard_map(
        body,
        mesh=mesh,
        in_specs=placed,
        out_specs=(P(None, ("tilt", "row"), "col"), P("tilt", None, None, None)),
        check_vma=False,
    )
```

profile of v0, /device:TPU:0, one launch (start us, length us, event | category | flops | bytes accessed | tf_op | source)
XLA Modules:
  0.0 179.6 jit_solution(4061278362378386647)
XLA Ops:
  7.2 4.9 %collective-permute-start = (f32[2,128,128]{2,1,0:T(8,128)}, f32[2,128,128]{2,1,0:T(8,128)S(1)}, u32[]{:S(2)}, u32[]{:S(2)}) collective-permute-start(f32[2,128,128]{2,1,0:T(8,128)} %param.23), channel_id=1, source_target_pairs={{0,2},{2,4},{4,6},{6,8},{8,10},{10,12},{12,14},{1,3},{3,5},{5,7},{... | collective-permute-start | bytes 393224 | tf_op jit(solution)/shard_map/ppermute | solution.py:17
  12.1 1.3 collective-permute-start.1
  13.4 1.7 collective-permute-done
  15.2 0.9 constant_dynamic-update-slice_fusion.1
  16.1 3.1 %collective-permute-done.1 = f32[2,128,128]{2,1,0:T(8,128)S(1)} collective-permute-done((f32[2,128,128]{2,1,0:T(8,128)}, f32[2,128,128]{2,1,0:T(8,128)S(1)}, u32[]{:S(2)}, u32[]{:S(2)}) %collective-permute-start.1) | collective-permute-done | bytes 131104 | tf_op jit(solution)/shard_map/ppermute | solution.py:20
  19.2 1.3 collective-permute-start.2
  20.5 1.3 collective-permute-start.3
  21.8 1.1 copy.41
  22.9 1.2 collective-permute-done.3
  24.1 1.1 pad_maximum_fusion
  25.3 0.8 copy-done.1
  26.1 42.0 %while.26 = (s32[]{:T(128)}, f32[2,384,384]{2,1,0:T(8,128)S(1)}, f32[4,2,128,128]{3,2,0,1:T(8,128)S(1)}, s32[1,1,2,2]{3,2,1,0:T(2,128)S(1)}, s32[]{:T(128)}, /*i...) while((s32[]{:T(128)}, f32[2,384,384]{2,1,0:T(8,128)S(1)}, ...), condition=%wide.region_4.5_spmd.clone.clone, body=%wide.region_0.4_spmd.clone.clone.sunk | while | flops 1617952768 | bytes 16646421 | solution.py:107
  30.7 1.1 dynamic-slice_bitcast_fusion.3
  44.8 2.2 %dynamic_update_slice.11 = f32[2,384,384]{2,1,0:T(8,128)S(1)} dynamic-update-slice(f32[2,384,384]{2,1,0:T(8,128)S(1)} %get-tuple-element.543, f32[2,128,128]{2,1,0:T(8,128)S(1)} %fusion.247, s32[]{:T(128)} %constant.191.clone.1..sunk, s32[]{:T(128)S(6)} %select_n.177, s32[]{:T(128)S(6)} %select_n.178) | dynamic-update-slice | bytes 262148 | tf_op jit(solution)/shard_map/while/body/eval_jaxpr/dynamic_update_slice | solution.py:103
  51.6 1.1 dynamic-slice_bitcast_fusion.3
  65.6 2.5 %dynamic_update_slice.11 = f32[2,384,384]{2,1,0:T(8,128)S(1)} dynamic-update-slice(f32[2,384,384]{2,1,0:T(8,128)S(1)} %get-tuple-element.543, f32[2,128,128]{2,1,0:T(8,128)S(1)} %fusion.247, s32[]{:T(128)} %constant.191.clone.1..sunk, s32[]{:T(128)S(6)} %select_n.177, s32[]{:T(128)S(6)} %select_n.178) | dynamic-update-slice | bytes 262148 | tf_op jit(solution)/shard_map/while/body/eval_jaxpr/dynamic_update_slice | solution.py:103
  69.0 4.5 %collective-permute-start.4 = (f32[2,128,384]{2,1,0:T(8,128)}, f32[2,128,384]{2,1,0:T(8,128)S(1)}, u32[]{:S(2)}, u32[]{:S(2)}) collective-permute-start(f32[2,128,384]{2,1,0:T(8,128)} %get-tuple-element.457), channel_id=1, source_target_pairs={{0,2},{2,4},{4,6},{6,8},{8,10},{10,12},{12,14},{1,3},{3,5},{5,7},{... | collective-permute-start | bytes 1179656 | tf_op jit(solution)/shard_map/ppermute | solution.py:17
  73.5 1.3 collective-permute-start.5
  76.1 0.8 copy.42
  77.0 14.1 %collective-permute-done.4 = f32[2,128,384]{2,1,0:T(8,128)S(1)} collective-permute-done((f32[2,128,384]{2,1,0:T(8,128)}, f32[2,128,384]{2,1,0:T(8,128)S(1)}, u32[]{:S(2)}, u32[]{:S(2)}) %collective-permute-start.4) | collective-permute-done | bytes 393248 | tf_op jit(solution)/shard_map/ppermute | solution.py:17
  91.1 1.4 collective-permute-start.6
  92.6 1.3 collective-permute-start.7
  93.9 76.3 %all-reduce.2.cloned.1.call-done = f32[4,2,128,128]{3,2,1,0:T(8,128)} async-done(((f32[4,2,128,128]{3,2,1,0:T(8,128)}), f32[4,2,128,128]{3,2,1,0:T(8,128)}) %all-reduce.2.cloned.1.call-update) | async-done | bytes 524304 | tf_op jit(solution)/shard_map/psum | solution.py:128
  170.2 1.9 %multiply_subtract_fusion = f32[4,2,128,128]{3,2,1,0:T(8,128)} fusion(f32[4,2,128,128]{3,2,1,0:T(8,128)S(1)} %copy-done, f32[4,2,128,128]{3,2,1,0:T(8,128)} %all-reduce.2.cloned.1.call-done), kind=kLoop, calls=%fused_computation.169 | loop fusion | flops 262144 | bytes 1572864 | tf_op jit(solution)/shard_map/sub | solution.py:129
  (63 shorter events, 28.0 us)
Async XLA Ops:
  7.2 163.0 %all-reduce.2.cloned.1.call-start = ((), (), s32[]{:S(2)}) async-start(), calls=%async_computation | async-start | bytes 1048576 | tf_op jit(solution)/shard_map/psum | solution.py:128
  7.2 7.9 %collective-permute-start = (f32[2,128,128]{2,1,0:T(8,128)}, f32[2,128,128]{2,1,0:T(8,128)S(1)}, u32[]{:S(2)}, u32[]{:S(2)}) collective-permute-start(f32[2,128,128]{2,1,0:T(8,128)} %param.23), channel_id=1, source_target_pairs={{0,2},{2,4},{4,6},{6,8},{8,10},{10,12},{12,14},{1,3},{3,5},{5,7},{... | collective-permute-start | bytes 393224 | tf_op jit(solution)/shard_map/ppermute | solution.py:17
  12.1 7.1 %collective-permute-start.1 = (f32[2,128,128]{2,1,0:T(8,128)}, f32[2,128,128]{2,1,0:T(8,128)S(1)}, u32[]{:S(2)}, u32[]{:S(2)}) collective-permute-start(f32[2,128,128]{2,1,0:T(8,128)} %param.23), channel_id=1, source_target_pairs={{2,0},{4,2},{6,4},{8,6},{10,8},{12,10},{14,12},{3,1},{5,3},{7,5},{... | collective-permute-start | bytes 393224 | tf_op jit(solution)/shard_map/ppermute | solution.py:20
  19.2 3.7 %collective-permute-start.2 = (f32[2,384,128]{2,1,0:T(8,128)S(1)}, f32[2,384,128]{2,1,0:T(8,128)S(1)}, u32[]{:S(2)}, u32[]{:S(2)}) collective-permute-start(f32[2,384,128]{2,1,0:T(8,128)S(1)} %constant_dynamic-update-slice_fusion), channel_id=1, source_target_pairs={{0,1},{2,3},{4,5},{6,7},{8,9},{10,11},{12,13},{14,15},{16,17},{18,... | collective-permute-start | bytes 1179656 | tf_op jit(solution)/shard_map/ppermute | solution.py:17
  20.5 3.6 %collective-permute-start.3 = (f32[2,384,128]{2,1,0:T(8,128)S(1)}, f32[2,384,128]{2,1,0:T(8,128)S(1)}, u32[]{:S(2)}, u32[]{:S(2)}) collective-permute-start(f32[2,384,128]{2,1,0:T(8,128)S(1)} %constant_dynamic-update-slice_fusion), channel_id=1, source_target_pairs={{1,0},{3,2},{5,4},{7,6},{9,8},{11,10},{13,12},{15,14},{17,16},{19,... | collective-permute-start | bytes 1179656 | tf_op jit(solution)/shard_map/ppermute | solution.py:20
  25.2 0.9 copy-start.1
  25.2 0.9 copy-start.3
  68.2 6.6 %copy-start = (f32[4,2,128,128]{3,2,1,0:T(8,128)S(1)}, f32[4,2,128,128]{3,2,1,0:T(8,128)}, u32[]{:S(2)}) copy-start(f32[4,2,128,128]{3,2,1,0:T(8,128)} %param.24) | copy-start | bytes 1572868
  69.0 22.0 %collective-permute-start.4 = (f32[2,128,384]{2,1,0:T(8,128)}, f32[2,128,384]{2,1,0:T(8,128)S(1)}, u32[]{:S(2)}, u32[]{:S(2)}) collective-permute-start(f32[2,128,384]{2,1,0:T(8,128)} %get-tuple-element.457), channel_id=1, source_target_pairs={{0,2},{2,4},{4,6},{6,8},{8,10},{10,12},{12,14},{1,3},{3,5},{5,7},{... | collective-permute-start | bytes 1179656 | tf_op jit(solution)/shard_map/ppermute | solution.py:17
  73.5 17.5 %collective-permute-start.5 = (f32[2,128,384]{2,1,0:T(8,128)S(1)}, f32[2,128,384]{2,1,0:T(8,128)S(1)}, u32[]{:S(2)}, u32[]{:S(2)}) collective-permute-start(f32[2,128,384]{2,1,0:T(8,128)S(1)} %get-tuple-element.458), channel_id=1, source_target_pairs={{2,0},{4,2},{6,4},{8,6},{10,8},{12,10},{14,12},{3,1},{5,3},{7,5},{... | collective-permute-start | bytes 1179656 | tf_op jit(solution)/shard_map/ppermute | solution.py:20
  91.1 81.0 %copy-start.2 = (f32[2,128,128]{2,1,0:T(8,128)S(1)}, f32[2,128,128]{2,1,0:T(8,128)}, u32[]{:S(2)}) copy-start(f32[2,128,128]{2,1,0:T(8,128)} %param.23) | copy-start | bytes 393220
  91.1 81.0 %collective-permute-start.6 = (f32[2,128,128]{2,1,0:T(8,128)S(1)}, f32[2,128,128]{2,1,0:T(8,128)S(1)}, u32[]{:S(2)}, u32[]{:S(2)}) collective-permute-start(f32[2,128,128]{2,1,0:T(8,128)S(1)} %get-tuple-element.459), channel_id=1, source_target_pairs={{0,1},{2,3},{4,5},{6,7},{8,9},{10,11},{12,13},{14,15},{16,17},{18,... | collective-permute-start | bytes 393224 | tf_op jit(solution)/shard_map/ppermute | solution.py:17
  92.6 79.5 %collective-permute-start.7 = (f32[2,128,128]{2,1,0:T(8,128)S(1)}, f32[2,128,128]{2,1,0:T(8,128)S(1)}, u32[]{:S(2)}, u32[]{:S(2)}) collective-permute-start(f32[2,128,128]{2,1,0:T(8,128)S(1)} %get-tuple-element.460), channel_id=1, source_target_pairs={{1,0},{3,2},{5,4},{7,6},{9,8},{11,10},{13,12},{15,14},{17,16},{19,... | collective-permute-start | bytes 393224 | tf_op jit(solution)/shard_map/ppermute | solution.py:20
Sparse Core Ops, SparseCore 0:
  77.1 93.0 all-reduce.1
where the time goes:
time: 180 us
  waiting for transfers between devices  96.5 us (54%)
  matrix products  23.8 us (13%)
  starting transfers between devices  17.3 us (10%)
  between operations  14.8 us (8%)
  local copies, waits for them, and re-layouts  12.6 us (7%)
  loops' own time  9.63 us (5%)
  other arithmetic  4.97 us (3%)
    psum x1, waiting for transfers between devices, body(): summed = lax.psum(probe_grad, ('row', 'col'))  76.3 us
    ppermute x4, waiting for transfers between devices, with_halo(): lax.ppermute(lax.slice_in_dim(block, block.shape[dim] - width, None, axis...  15.8 us
    ppermute x4, starting transfers between devices, with_halo(): lax.ppermute(lax.slice_in_dim(block, block.shape[dim] - width, None, axis...  12.1 us
    another operation x1, loops' own time, body(): gradient, probe_grad = lax.fori_loop(0, slot_total, slot_step, start_carry)  9.63 us
    ppermute x4, starting transfers between devices, with_halo(): lax.ppermute(lax.slice_in_dim(block, 0, width, axis=dim), axis, backward)  5.17 us
    dynamic_update_slice x2, local copies, waits for them, and re-layouts, slot_step(): lax.dynamic_update_slice(local_grad, region, (as_index(0), corner_y, corn...  4.66 us
    ppermute x4, waiting for transfers between devices, with_halo(): lax.ppermute(lax.slice_in_dim(block, 0, width, axis=dim), axis, backward)  4.31 us
  transfers between devices with their start and end apart: 9, of which 5 were waited for; matrix products, arithmetic and copies ran while one was open for 3% of the time, Pallas kernels for 0%

commit v1 on v0

--- a/solution.py
+++ b/solution.py
@@ -125,7 +125,7 @@
         jnp.max(jnp.sum(probe[:, 0] * probe[:, 0] + probe[:, 1] * probe[:, 1], axis=0)) + epsilon
     )
     object_field = object_field - object_rate * object_grad / weight
-    summed = lax.psum(probe_grad, ("row", "col"))
+    summed = jnp.sum(lax.all_gather(probe_grad, ("row", "col")), axis=0)
     probe = probe - probe_rate * summed / tile_total
     return (object_field, probe)
 

time: 180 us -> 165 us (0.917)
  waiting for transfers between devices: 96.5 us -> 80 us
  other arithmetic: 4.97 us -> 7.09 us
    psum x1 -> x0, waiting for transfers between devices: 76.3 us -> none  [body(): summed = lax.psum(probe_grad, ('row', 'col'))]
    all_gather x0 -> x1, waiting for transfers between devices: none -> 52.9 us  [body(): summed = jnp.sum(lax.all_gather(probe_grad, ('row', 'col')), axis=0)]
    ppermute x4, waiting for transfers between devices: 15.8 us -> 22.2 us  [with_halo(): lax.ppermute(lax.slice_in_dim(block, block.shape[dim] - width, None, axis...]
    reduce_sum x0 -> x1, other arithmetic: none -> 3.94 us  [body(): summed = jnp.sum(lax.all_gather(probe_grad, ('row', 'col')), axis=0)]
    sub x1, other arithmetic: 1.89 us -> 0.06 us  [body(): probe = probe - probe_rate * summed / tile_total]
    unnamed x11 -> x14, local copies, waits for them, and re-layouts: 2.84 us -> 4.46 us
  transfers between devices with their start and end apart: 9 -> 9, of which waited for: 5 -> 6; matrix products, arithmetic and copies ran while one was open for 3% -> 2% of each run, Pallas kernels for 0% -> 0%
where the time goes in v1:
time: 165 us
  waiting for transfers between devices  80 us (48%)
  matrix products  23.8 us (14%)
  starting transfers between devices  17.5 us (11%)
  between operations  14.9 us (9%)
  local copies, waits for them, and re-layouts  12.6 us (8%)
  loops' own time  8.91 us (5%)
  other arithmetic  7.09 us (4%)
    all_gather x1, waiting for transfers between devices, body(): summed = jnp.sum(lax.all_gather(probe_grad, ('row', 'col')), axis=0)  52.9 us
    ppermute x4, waiting for transfers between devices, with_halo(): lax.ppermute(lax.slice_in_dim(block, block.shape[dim] - width, None, axis...  22.2 us
    ppermute x4, starting transfers between devices, with_halo(): lax.ppermute(lax.slice_in_dim(block, block.shape[dim] - width, None, axis...  12.1 us
    another operation x1, loops' own time, body(): gradient, probe_grad = lax.fori_loop(0, slot_total, slot_step, start_carry)  8.91 us
    ppermute x4, starting transfers between devices, with_halo(): lax.ppermute(lax.slice_in_dim(block, 0, width, axis=dim), axis, backward)  5.3 us
    ppermute x4, waiting for transfers between devices, with_halo(): lax.ppermute(lax.slice_in_dim(block, 0, width, axis=dim), axis, backward)  4.92 us
    dynamic_update_slice x2, local copies, waits for them, and re-layouts, slot_step(): lax.dynamic_update_slice(local_grad, region, (as_index(0), corner_y, corn...  4.66 us
    unnamed x14, local copies, waits for them, and re-layouts  4.46 us
  transfers between devices with their start and end apart: 9, of which 6 were waited for; matrix products, arithmetic and copies ran while one was open for 2% of the time, Pallas kernels for 0%

profile of v1, /device:TPU:0, one launch (start us, length us, event | category | flops | bytes accessed | tf_op | source)
XLA Modules:
  0.0 164.8 jit_solution(12804561972044171489)
XLA Ops:
  7.2 4.9 %collective-permute-start = (f32[2,128,128]{2,1,0:T(8,128)}, f32[2,128,128]{2,1,0:T(8,128)S(1)}, u32[]{:S(2)}, u32[]{:S(2)}) collective-permute-start(f32[2,128,128]{2,1,0:T(8,128)} %param.23), channel_id=1, source_target_pairs={{0,2},{2,4},{4,6},{6,8},{8,10},{10,12},{12,14},{1,3},{3,5},{5,7},{... | collective-permute-start | bytes 393224 | tf_op jit(solution)/shard_map/ppermute | solution.py:17
  12.1 1.3 collective-permute-start.1
  13.4 1.7 %collective-permute-done = f32[2,128,128]{2,1,0:T(8,128)S(1)} collective-permute-done((f32[2,128,128]{2,1,0:T(8,128)}, f32[2,128,128]{2,1,0:T(8,128)S(1)}, u32[]{:S(2)}, u32[]{:S(2)}) %collective-permute-start) | collective-permute-done | bytes 131104 | tf_op jit(solution)/shard_map/ppermute | solution.py:17
  15.2 0.9 constant_dynamic-update-slice_fusion.1
  16.1 3.1 %collective-permute-done.1 = f32[2,128,128]{2,1,0:T(8,128)S(1)} collective-permute-done((f32[2,128,128]{2,1,0:T(8,128)}, f32[2,128,128]{2,1,0:T(8,128)S(1)}, u32[]{:S(2)}, u32[]{:S(2)}) %collective-permute-start.1) | collective-permute-done | bytes 131104 | tf_op jit(solution)/shard_map/ppermute | solution.py:20
  19.2 1.3 collective-permute-start.2
  20.5 1.3 collective-permute-start.3
  21.8 1.1 copy.59
  22.9 1.2 collective-permute-done.3
  24.1 1.1 pad_maximum_fusion
  25.3 0.8 copy-done.2
  26.1 41.3 %while.26 = (s32[]{:T(128)}, f32[2,384,384]{2,1,0:T(8,128)S(1)}, f32[4,2,128,128]{3,2,0,1:T(8,128)S(1)}, s32[1,1,2,2]{3,2,1,0:T(2,128)S(1)}, s32[]{:T(128)}, /*i...) while((s32[]{:T(128)}, f32[2,384,384]{2,1,0:T(8,128)S(1)}, ...), condition=%wide.region_4.5_spmd.clone.clone, body=%wide.region_0.4_spmd.clone.clone.sunk | while | flops 1617952768 | bytes 16646421 | solution.py:107
  30.4 1.1 dynamic-slice_bitcast_fusion.3
  44.4 2.2 %dynamic_update_slice.11 = f32[2,384,384]{2,1,0:T(8,128)S(1)} dynamic-update-slice(f32[2,384,384]{2,1,0:T(8,128)S(1)} %get-tuple-element.555, f32[2,128,128]{2,1,0:T(8,128)S(1)} %fusion.247, s32[]{:T(128)} %constant.191.clone.1..sunk, s32[]{:T(128)S(6)} %select_n.177, s32[]{:T(128)S(6)} %select_n.178) | dynamic-update-slice | bytes 262148 | tf_op jit(solution)/shard_map/while/body/eval_jaxpr/dynamic_update_slice | solution.py:103
  50.8 1.1 dynamic-slice_bitcast_fusion.3
  64.9 2.5 %dynamic_update_slice.11 = f32[2,384,384]{2,1,0:T(8,128)S(1)} dynamic-update-slice(f32[2,384,384]{2,1,0:T(8,128)S(1)} %get-tuple-element.555, f32[2,128,128]{2,1,0:T(8,128)S(1)} %fusion.247, s32[]{:T(128)} %constant.191.clone.1..sunk, s32[]{:T(128)S(6)} %select_n.177, s32[]{:T(128)S(6)} %select_n.178) | dynamic-update-slice | bytes 262148 | tf_op jit(solution)/shard_map/while/body/eval_jaxpr/dynamic_update_slice | solution.py:103
  68.3 4.6 %collective-permute-start.4 = (f32[2,128,384]{2,1,0:T(8,128)S(1)}, f32[2,128,384]{2,1,0:T(8,128)S(1)}, u32[]{:S(2)}, u32[]{:S(2)}) collective-permute-start(f32[2,128,384]{2,1,0:T(8,128)S(1)} %get-tuple-element.469), channel_id=1, source_target_pairs={{0,2},{2,4},{4,6},{6,8},{8,10},{10,12},{12,14},{1,3},{3,5},{5,7},{... | collective-permute-start | bytes 1179656 | tf_op jit(solution)/shard_map/ppermute | solution.py:17
  73.0 1.4 collective-permute-start.5
  74.4 20.5 %collective-permute-done.4 = f32[2,128,384]{2,1,0:T(8,128)S(1)} collective-permute-done((f32[2,128,384]{2,1,0:T(8,128)S(1)}, f32[2,128,384]{2,1,0:T(8,128)S(1)}, u32[]{:S(2)}, u32[]{:S(2)}) %collective-permute-start.4) | collective-permute-done | bytes 393248 | tf_op jit(solution)/shard_map/ppermute | solution.py:17
  95.0 1.3 collective-permute-start.6
  96.3 1.3 collective-permute-start.7
  100.2 52.9 %all-gather.3.cloned.1.call-done = f32[64,2,128,128]{3,2,0,1:T(8,128)} async-done(((f32[4,2,128,128]{3,2,0,1:T(8,128)}), f32[64,2,128,128]{3,2,0,1:T(8,128)}) %all-gather.3.cloned.1.call-update) | async-done | bytes 8388624 | tf_op jit(solution)/shard_map/all_gather | solution.py:128
  153.1 3.9 %reduce_sum.61 = f32[4,2,128,128]{3,2,0,1:T(8,128)S(1)} reduce(f32[16,4,2,128,128]{4,3,1,0,2:T(8,128)} %bitcast.195, f32[]{:T(128)} %constant.192.clone.1), dimensions={0}, to_apply=%region_7.8 | reduce | flops 1966080 | bytes 8912900 | tf_op jit(solution)/shard_map/reduce_sum | solution.py:128
  157.1 0.8 copy.61
  (66 shorter events, 28.7 us)
Async XLA Ops:
  7.2 145.9 %all-gather.3.cloned.1.call-start = ((), (), s32[]{:S(2)}) async-start(), calls=%async_computation | async-start | bytes 8912896 | tf_op jit(solution)/shard_map/all_gather | solution.py:128
  7.2 7.9 %collective-permute-start = (f32[2,128,128]{2,1,0:T(8,128)}, f32[2,128,128]{2,1,0:T(8,128)S(1)}, u32[]{:S(2)}, u32[]{:S(2)}) collective-permute-start(f32[2,128,128]{2,1,0:T(8,128)} %param.23), channel_id=1, source_target_pairs={{0,2},{2,4},{4,6},{6,8},{8,10},{10,12},{12,14},{1,3},{3,5},{5,7},{... | collective-permute-start | bytes 393224 | tf_op jit(solution)/shard_map/ppermute | solution.py:17
  12.1 7.1 %collective-permute-start.1 = (f32[2,128,128]{2,1,0:T(8,128)}, f32[2,128,128]{2,1,0:T(8,128)S(1)}, u32[]{:S(2)}, u32[]{:S(2)}) collective-permute-start(f32[2,128,128]{2,1,0:T(8,128)} %param.23), channel_id=1, source_target_pairs={{2,0},{4,2},{6,4},{8,6},{10,8},{12,10},{14,12},{3,1},{5,3},{7,5},{... | collective-permute-start | bytes 393224 | tf_op jit(solution)/shard_map/ppermute | solution.py:20
  19.2 3.7 %collective-permute-start.2 = (f32[2,384,128]{2,1,0:T(8,128)S(1)}, f32[2,384,128]{2,1,0:T(8,128)S(1)}, u32[]{:S(2)}, u32[]{:S(2)}) collective-permute-start(f32[2,384,128]{2,1,0:T(8,128)S(1)} %constant_dynamic-update-slice_fusion), channel_id=1, source_target_pairs={{0,1},{2,3},{4,5},{6,7},{8,9},{10,11},{12,13},{14,15},{16,17},{18,... | collective-permute-start | bytes 1179656 | tf_op jit(solution)/shard_map/ppermute | solution.py:17
  20.5 3.6 %collective-permute-start.3 = (f32[2,384,128]{2,1,0:T(8,128)S(1)}, f32[2,384,128]{2,1,0:T(8,128)S(1)}, u32[]{:S(2)}, u32[]{:S(2)}) collective-permute-start(f32[2,384,128]{2,1,0:T(8,128)S(1)} %constant_dynamic-update-slice_fusion), channel_id=1, source_target_pairs={{1,0},{3,2},{5,4},{7,6},{9,8},{11,10},{13,12},{15,14},{17,16},{19,... | collective-permute-start | bytes 1179656 | tf_op jit(solution)/shard_map/ppermute | solution.py:20
  25.2 0.9 copy-start.2
  25.2 0.9 copy-start.4
  67.4 0.8 copy-start
  68.3 29.3 %copy-start.1 = (f32[4,2,128,128]{3,2,1,0:T(8,128)S(1)}, f32[4,2,128,128]{3,2,1,0:T(8,128)}, u32[]{:S(2)}) copy-start(f32[4,2,128,128]{3,2,1,0:T(8,128)} %param.24) | copy-start | bytes 1572868
  68.3 26.6 %collective-permute-start.4 = (f32[2,128,384]{2,1,0:T(8,128)S(1)}, f32[2,128,384]{2,1,0:T(8,128)S(1)}, u32[]{:S(2)}, u32[]{:S(2)}) collective-permute-start(f32[2,128,384]{2,1,0:T(8,128)S(1)} %get-tuple-element.469), channel_id=1, source_target_pairs={{0,2},{2,4},{4,6},{6,8},{8,10},{10,12},{12,14},{1,3},{3,5},{5,7},{... | collective-permute-start | bytes 1179656 | tf_op jit(solution)/shard_map/ppermute | solution.py:17
  73.0 26.6 %copy-start.3 = (f32[2,128,128]{2,1,0:T(8,128)S(1)}, f32[2,128,128]{2,1,0:T(8,128)}, u32[]{:S(2)}) copy-start(f32[2,128,128]{2,1,0:T(8,128)} %param.23) | copy-start | bytes 393220
  73.0 21.9 %collective-permute-start.5 = (f32[2,128,384]{2,1,0:T(8,128)S(1)}, f32[2,128,384]{2,1,0:T(8,128)S(1)}, u32[]{:S(2)}, u32[]{:S(2)}) collective-permute-start(f32[2,128,384]{2,1,0:T(8,128)S(1)} %get-tuple-element.470), channel_id=1, source_target_pairs={{2,0},{4,2},{6,4},{8,6},{10,8},{12,10},{14,12},{3,1},{5,3},{7,5},{... | collective-permute-start | bytes 1179656 | tf_op jit(solution)/shard_map/ppermute | solution.py:20
  95.0 3.9 %collective-permute-start.6 = (f32[2,128,128]{2,1,0:T(8,128)S(1)}, f32[2,128,128]{2,1,0:T(8,128)S(1)}, u32[]{:S(2)}, u32[]{:S(2)}) collective-permute-start(f32[2,128,128]{2,1,0:T(8,128)S(1)} %get-tuple-element.471), channel_id=1, source_target_pairs={{0,1},{2,3},{4,5},{6,7},{8,9},{10,11},{12,13},{14,15},{16,17},{18,... | collective-permute-start | bytes 393224 | tf_op jit(solution)/shard_map/ppermute | solution.py:17
  96.3 3.2 %collective-permute-start.7 = (f32[2,128,128]{2,1,0:T(8,128)S(1)}, f32[2,128,128]{2,1,0:T(8,128)S(1)}, u32[]{:S(2)}, u32[]{:S(2)}) collective-permute-start(f32[2,128,128]{2,1,0:T(8,128)S(1)} %get-tuple-element.472), channel_id=1, source_target_pairs={{1,0},{3,2},{5,4},{7,6},{9,8},{11,10},{13,12},{15,14},{17,16},{19,... | collective-permute-start | bytes 393224 | tf_op jit(solution)/shard_map/ppermute | solution.py:20
Sparse Core Ops, SparseCore 0:
  68.4 84.6 all-gather.2
